TPU v7x, 32 devices: a whole 2x2x4 slice. The times are simulated.
32 devices in a mesh: stn: 8 (over z, x), pts: 2 (over core), freq: 2 (over y).
Axes of the slice: x: 2, y: 2, z: 4, core: 2. Of those that a mesh axis runs over, the one named last changes fastest.
Arguments:
- greens: bfloat16 [2, 4, 2048, 4096], P(None, 'freq', 'stn', 'pts'), may hold values from -6 to 6
- noise_weights: bfloat16 [2, 4, 2048, 2048], P(None, 'freq', 'stn'), may hold values from -12 to 12, as said below
Outputs:
- kernel: float32 [4096], P('pts')
Inputs may be any that keep to these rules, and one draw needn't show every extreme that they name: For every frequency, noise_weights[0] is symmetric and noise_weights[1] antisymmetric in the two station dimensions, so each frequency's matrix is Hermitian.
All inputs are finite; a program needn't handle non-finite values. Where the computation divides by a largest or mean magnitude, that divisor is 1e-20 or more.
Results may differ from a plain program's by a relative error of at most 0.0003.
Values may be sent and summed in bfloat16 or wider, within the bound.
A program may use at most 192 MiB of HBM per device.

v0:
```python
import jax
import jax.numpy as jnp
from jax import lax
from jax.sharding import PartitionSpec as P


def passed_along(x, axis, by):
    size = lax.axis_size(axis)
    return lax.ppermute(x, axis, [(i, (i + by) % size) for i in range(size)])


def mixing_of(weights):
    negated = -weights[1]
    return jnp.stack([jnp.stack([weights[0], negated]), jnp.stack([weights[1], weights[0]])])


def body(greens, noise_weights):
    station_rows = greens.shape[2]
    stations = noise_weights.shape[3]
    device_index = lax.axis_index("stn")
    cycle_length = lax.axis_size("stn")
    mixing = mixing_of(noise_weights)

    def block_product(columns_start, arriving):
        block_rows = arriving.shape[2]
        weights_block = lax.dynamic_slice_in_dim(mixing, columns_start, block_rows, 4)
        return jnp.einsum(
            "ocfin,cfnx->ofix", weights_block, arriving, preferred_element_type=jnp.float32
        )

    half_way = cycle_length // 2
    diagonal = block_product(device_index * station_rows, greens)

    def advance(offset, loop_state):
        running, current = loop_state
        current = passed_along(current, "stn", -1)
        source = (device_index + offset) % cycle_length
        weight = jnp.where(offset == half_way, 1.0, 2.0).astype(jnp.float32)
        running = running + weight * block_product(source * station_rows, current)
        return (running, current)

    summed, current = lax.fori_loop(1, half_way + 1, advance, (diagonal, greens))
    green_real = greens[0].astype(jnp.float32)
    green_imag = greens[1].astype(jnp.float32)
    partial_kernel = (
        jnp.sum(green_real * summed[0] + green_imag * summed[1], axis=(0, 1)) / stations
    )
    raw_kernel = lax.psum(partial_kernel, "stn")
    raw_kernel = lax.psum(raw_kernel, "freq")
    largest = lax.pmax(jnp.max(jnp.abs(raw_kernel)), "pts")
    return raw_kernel / (largest + 1e-06)


def solution(mesh):
    in_specs = (P(None, "freq", "stn", "pts"), P(None, "freq", "stn", None))
    out_specs = P("pts")
    return jax.shard_map(body, mesh=mesh, in_specs=in_specs, out_specs=out_specs, check_vma=False)
```

profile of v0, /device:TPU:0, one launch (start us, length us, event | category | flops | bytes accessed | tf_op | source)
XLA Modules:
  0.0 490.5 jit_solution(11815002905241428703)
XLA Ops:
  9.8 5.6 %convolution_bitcast_fusion = f32[2,2,256,2048]{3,2,0,1:T(8,128)} fusion(s32[]{:T(128)S(6)} %select_n.44, bf16[1,2,2,256,2048]{4,3,1,0,2:T(8,128)(2,1)S(1)} %get-tuple-element.157, bf16[1,2,2,256,2048]{4,3,1,0,2:T(8,128)(2,1)S(1)} %get-tuple-element.156, bf16[2,2,256,2048]{3,2,1,0:T(8,128)(2,1)S(1)} %copy-done.3), kind=kOutput, calls=%fused_computation.8 | convolution fusion | flops 2149580800 | bytes 20971524 | tf_op jit(solution)/shard_map/ocfin,cfnx->ofix/dot_general | solution.py:27
  15.4 6.2 %pad_maximum_fusion = bf16[2,2,2,256,2048]{4,3,1,0,2:T(8,128)(2,1)} fusion(bf16[1,2,2,256,2048]{4,3,1,0,2:T(8,128)(2,1)S(1)} %get-tuple-element.156, bf16[1,2,2,256,2048]{4,3,1,0,2:T(8,128)(2,1)} %copy-done.2), kind=kLoop, calls=%fused_computation.6 | loop fusion | flops 4194304 | bytes 16777216 | tf_op jit(solution)/shard_map/stack | solution.py:14
  21.6 431.1 %while.17 = (s32[]{:T(128)}, f32[2,2,256,2048]{3,2,0,1:T(8,128)}, bf16[2,2,256,2048]{3,2,0,1:T(8,128)(2,1)}, s32[]{:T(128)}, bf16[2,2,2,256,2048]{4,3,1,0,2:T(8,...) while((s32[]{:T(128)}, f32[2,2,256,2048]{3,2,0,1:T(8,128)}, ...), condition=%wide.region_1.2_spmd, body=%wide.region_0.1_spmd.sunk | while | flops 2151677952 | bytes 114295200 | solution.py:42
  21.6 6.0 %collective-permute-start = (bf16[2,2,256,2048]{3,2,0,1:T(8,128)(2,1)}, bf16[2,2,256,2048]{3,2,0,1:T(8,128)(2,1)}, u32[]{:S(2)}, u32[]{:S(2)}) collective-permute-start(bf16[2,2,256,2048]{3,2,0,1:T(8,128)(2,1)} %get-tuple-element.205), channel_id=1, source_target_pairs={{0,28},{4,0},{8,4},{12,8},{16,12},{20,16},{24,20},{28,24},{1,29},{... | collective-permute-start | bytes 12582920 | tf_op jit(solution)/shard_map/while/body/eval_jaxpr/ppermute | solution.py:9
  27.6 90.1 %collective-permute-done = bf16[2,2,256,2048]{3,2,0,1:T(8,128)(2,1)} collective-permute-done((bf16[2,2,256,2048]{3,2,0,1:T(8,128)(2,1)}, bf16[2,2,256,2048]{3,2,0,1:T(8,128)(2,1)}, u32[]{:S(2)}, u32[]{:S(2)}) %collective-permute-start) | collective-permute-done | bytes 4194336 | tf_op jit(solution)/shard_map/while/body/eval_jaxpr/ppermute | solution.py:9
  117.7 4.7 copy.30
  122.4 5.6 %bitcast_add_fusion.2 = f32[2,2,256,2048]{3,2,0,1:T(8,128)S(1)} fusion(f32[2,2,256,2048]{3,2,0,1:T(8,128)S(1)} %copy-done, bf16[2,2,256,2048]{3,2,0,1:T(8,128)(2,1)} %collective-permute-done, f32[]{:T(128)S(6)} %select_n.48, bf16[2,2,2,256,2048]{4,3,1,0,2:T(8,128)(2,1)} %get-tuple-element.221, s32[]{:T(128)S(6)} %select_n.50), kind=kOutput, calls=%fused_computation.clone.1 | convolution fusion | flops 2151677952 | bytes 22020104 | tf_op jit(solution)/shard_map/while/body/eval_jaxpr/ocfin,cfnx->ofix/dot_general | solution.py:27
  128.1 3.2 copy-done.1
  131.3 5.2 %collective-permute-start = (bf16[2,2,256,2048]{3,2,0,1:T(8,128)(2,1)}, bf16[2,2,256,2048]{3,2,0,1:T(8,128)(2,1)}, u32[]{:S(2)}, u32[]{:S(2)}) collective-permute-start(bf16[2,2,256,2048]{3,2,0,1:T(8,128)(2,1)} %get-tuple-element.205), channel_id=1, source_target_pairs={{0,28},{4,0},{8,4},{12,8},{16,12},{20,16},{24,20},{28,24},{1,29},{... | collective-permute-start | bytes 12582920 | tf_op jit(solution)/shard_map/while/body/eval_jaxpr/ppermute | solution.py:9
  136.4 89.3 %collective-permute-done = bf16[2,2,256,2048]{3,2,0,1:T(8,128)(2,1)} collective-permute-done((bf16[2,2,256,2048]{3,2,0,1:T(8,128)(2,1)}, bf16[2,2,256,2048]{3,2,0,1:T(8,128)(2,1)}, u32[]{:S(2)}, u32[]{:S(2)}) %collective-permute-start) | collective-permute-done | bytes 4194336 | tf_op jit(solution)/shard_map/while/body/eval_jaxpr/ppermute | solution.py:9
  225.7 4.7 copy.30
  230.4 5.6 %bitcast_add_fusion.2 = f32[2,2,256,2048]{3,2,0,1:T(8,128)S(1)} fusion(f32[2,2,256,2048]{3,2,0,1:T(8,128)S(1)} %copy-done, bf16[2,2,256,2048]{3,2,0,1:T(8,128)(2,1)} %collective-permute-done, f32[]{:T(128)S(6)} %select_n.48, bf16[2,2,2,256,2048]{4,3,1,0,2:T(8,128)(2,1)} %get-tuple-element.221, s32[]{:T(128)S(6)} %select_n.50), kind=kOutput, calls=%fused_computation.clone.1 | convolution fusion | flops 2151677952 | bytes 22020104 | tf_op jit(solution)/shard_map/while/body/eval_jaxpr/ocfin,cfnx->ofix/dot_general | solution.py:27
  236.0 3.2 copy-done.1
  239.2 5.2 %collective-permute-start = (bf16[2,2,256,2048]{3,2,0,1:T(8,128)(2,1)}, bf16[2,2,256,2048]{3,2,0,1:T(8,128)(2,1)}, u32[]{:S(2)}, u32[]{:S(2)}) collective-permute-start(bf16[2,2,256,2048]{3,2,0,1:T(8,128)(2,1)} %get-tuple-element.205), channel_id=1, source_target_pairs={{0,28},{4,0},{8,4},{12,8},{16,12},{20,16},{24,20},{28,24},{1,29},{... | collective-permute-start | bytes 12582920 | tf_op jit(solution)/shard_map/while/body/eval_jaxpr/ppermute | solution.py:9
  244.4 88.4 %collective-permute-done = bf16[2,2,256,2048]{3,2,0,1:T(8,128)(2,1)} collective-permute-done((bf16[2,2,256,2048]{3,2,0,1:T(8,128)(2,1)}, bf16[2,2,256,2048]{3,2,0,1:T(8,128)(2,1)}, u32[]{:S(2)}, u32[]{:S(2)}) %collective-permute-start) | collective-permute-done | bytes 4194336 | tf_op jit(solution)/shard_map/while/body/eval_jaxpr/ppermute | solution.py:9
  332.8 4.7 copy.30
  337.5 5.6 %bitcast_add_fusion.2 = f32[2,2,256,2048]{3,2,0,1:T(8,128)S(1)} fusion(f32[2,2,256,2048]{3,2,0,1:T(8,128)S(1)} %copy-done, bf16[2,2,256,2048]{3,2,0,1:T(8,128)(2,1)} %collective-permute-done, f32[]{:T(128)S(6)} %select_n.48, bf16[2,2,2,256,2048]{4,3,1,0,2:T(8,128)(2,1)} %get-tuple-element.221, s32[]{:T(128)S(6)} %select_n.50), kind=kOutput, calls=%fused_computation.clone.1 | convolution fusion | flops 2151677952 | bytes 22020104 | tf_op jit(solution)/shard_map/while/body/eval_jaxpr/ocfin,cfnx->ofix/dot_general | solution.py:27
  346.4 5.2 %collective-permute-start = (bf16[2,2,256,2048]{3,2,0,1:T(8,128)(2,1)}, bf16[2,2,256,2048]{3,2,0,1:T(8,128)(2,1)}, u32[]{:S(2)}, u32[]{:S(2)}) collective-permute-start(bf16[2,2,256,2048]{3,2,0,1:T(8,128)(2,1)} %get-tuple-element.205), channel_id=1, source_target_pairs={{0,28},{4,0},{8,4},{12,8},{16,12},{20,16},{24,20},{28,24},{1,29},{... | collective-permute-start | bytes 12582920 | tf_op jit(solution)/shard_map/while/body/eval_jaxpr/ppermute | solution.py:9
  351.6 87.6 %collective-permute-done = bf16[2,2,256,2048]{3,2,0,1:T(8,128)(2,1)} collective-permute-done((bf16[2,2,256,2048]{3,2,0,1:T(8,128)(2,1)}, bf16[2,2,256,2048]{3,2,0,1:T(8,128)(2,1)}, u32[]{:S(2)}, u32[]{:S(2)}) %collective-permute-start) | collective-permute-done | bytes 4194336 | tf_op jit(solution)/shard_map/while/body/eval_jaxpr/ppermute | solution.py:9
  439.1 4.7 copy.30
  443.8 5.6 %bitcast_add_fusion.2 = f32[2,2,256,2048]{3,2,0,1:T(8,128)S(1)} fusion(f32[2,2,256,2048]{3,2,0,1:T(8,128)S(1)} %copy-done, bf16[2,2,256,2048]{3,2,0,1:T(8,128)(2,1)} %collective-permute-done, f32[]{:T(128)S(6)} %select_n.48, bf16[2,2,2,256,2048]{4,3,1,0,2:T(8,128)(2,1)} %get-tuple-element.221, s32[]{:T(128)S(6)} %select_n.50), kind=kOutput, calls=%fused_computation.clone.1 | convolution fusion | flops 2151677952 | bytes 22020104 | tf_op jit(solution)/shard_map/while/body/eval_jaxpr/ocfin,cfnx->ofix/dot_general | solution.py:27
  452.6 5.3 %add_reduce_fusion = f32[2048]{0:T(1024)S(1)} fusion(f32[2,2,256,2048]{3,2,0,1:T(8,128)} %get-tuple-element.138, bf16[2,2,256,2048]{3,2,1,0:T(8,128)(2,1)} %param.4), kind=kLoop, calls=%fused_computation.12 | loop fusion | flops 6289408 | bytes 12591104 | tf_op jit(solution)/shard_map/reduce_sum | solution.py:46
  458.0 22.6 %psum.14 = f32[2048]{0:T(1024)S(1)} all-reduce(f32[2048]{0:T(1024)S(1)} %broadcast_multiply_fusion), channel_id=1, replica_groups=mesh['stn'=8,'pts'=2,'freq'=2] {'stn'}, use_global_device_ids=true, to_apply=%region_3.4 | all-reduce | flops 2048 | bytes 16384 | tf_op jit(solution)/shard_map/psum | solution.py:48
  480.5 5.0 %psum.15 = f32[2048]{0:T(1024)S(1)} all-reduce(f32[2048]{0:T(1024)S(1)} %psum.14), channel_id=1, replica_groups=mesh['stn'=8,'pts'=2,'freq'=2] {'freq'}, use_global_device_ids=true, to_apply=%region_4.5 | all-reduce | flops 2048 | bytes 16384 | tf_op jit(solution)/shard_map/psum | solution.py:49
  (28 shorter events, 20.5 us)
Async XLA Ops:
  0.0 2.8 copy-start.3
  2.8 3.7 copy-start.4
  7.8 2.0 copy-start.2
  21.6 96.2 %collective-permute-start = (bf16[2,2,256,2048]{3,2,0,1:T(8,128)(2,1)}, bf16[2,2,256,2048]{3,2,0,1:T(8,128)(2,1)}, u32[]{:S(2)}, u32[]{:S(2)}) collective-permute-start(bf16[2,2,256,2048]{3,2,0,1:T(8,128)(2,1)} %get-tuple-element.205), channel_id=1, source_target_pairs={{0,28},{4,0},{8,4},{12,8},{16,12},{20,16},{24,20},{28,24},{1,29},{... | collective-permute-start | bytes 12582920 | tf_op jit(solution)/shard_map/while/body/eval_jaxpr/ppermute | solution.py:9
  27.6 94.8 %copy-start = (f32[2,2,256,2048]{3,2,0,1:T(8,128)S(1)}, f32[2,2,256,2048]{3,2,0,1:T(8,128)}, u32[]{:S(2)}) copy-start(f32[2,2,256,2048]{3,2,0,1:T(8,128)} %get-tuple-element.204) | copy-start | bytes 25165828 | tf_op jit(solution)/shard_map/while
  128.1 3.2 copy-start.1
  131.3 94.5 %collective-permute-start = (bf16[2,2,256,2048]{3,2,0,1:T(8,128)(2,1)}, bf16[2,2,256,2048]{3,2,0,1:T(8,128)(2,1)}, u32[]{:S(2)}, u32[]{:S(2)}) collective-permute-start(bf16[2,2,256,2048]{3,2,0,1:T(8,128)(2,1)} %get-tuple-element.205), channel_id=1, source_target_pairs={{0,28},{4,0},{8,4},{12,8},{16,12},{20,16},{24,20},{28,24},{1,29},{... | collective-permute-start | bytes 12582920 | tf_op jit(solution)/shard_map/while/body/eval_jaxpr/ppermute | solution.py:9
  136.4 94.0 %copy-start = (f32[2,2,256,2048]{3,2,0,1:T(8,128)S(1)}, f32[2,2,256,2048]{3,2,0,1:T(8,128)}, u32[]{:S(2)}) copy-start(f32[2,2,256,2048]{3,2,0,1:T(8,128)} %get-tuple-element.204) | copy-start | bytes 25165828 | tf_op jit(solution)/shard_map/while
  236.0 3.2 copy-start.1
  239.2 93.6 %collective-permute-start = (bf16[2,2,256,2048]{3,2,0,1:T(8,128)(2,1)}, bf16[2,2,256,2048]{3,2,0,1:T(8,128)(2,1)}, u32[]{:S(2)}, u32[]{:S(2)}) collective-permute-start(bf16[2,2,256,2048]{3,2,0,1:T(8,128)(2,1)} %get-tuple-element.205), channel_id=1, source_target_pairs={{0,28},{4,0},{8,4},{12,8},{16,12},{20,16},{24,20},{28,24},{1,29},{... | collective-permute-start | bytes 12582920 | tf_op jit(solution)/shard_map/while/body/eval_jaxpr/ppermute | solution.py:9
  244.4 93.1 %copy-start = (f32[2,2,256,2048]{3,2,0,1:T(8,128)S(1)}, f32[2,2,256,2048]{3,2,0,1:T(8,128)}, u32[]{:S(2)}) copy-start(f32[2,2,256,2048]{3,2,0,1:T(8,128)} %get-tuple-element.204) | copy-start | bytes 25165828 | tf_op jit(solution)/shard_map/while
  343.2 3.2 copy-start.1
  346.4 92.7 %collective-permute-start = (bf16[2,2,256,2048]{3,2,0,1:T(8,128)(2,1)}, bf16[2,2,256,2048]{3,2,0,1:T(8,128)(2,1)}, u32[]{:S(2)}, u32[]{:S(2)}) collective-permute-start(bf16[2,2,256,2048]{3,2,0,1:T(8,128)(2,1)} %get-tuple-element.205), channel_id=1, source_target_pairs={{0,28},{4,0},{8,4},{12,8},{16,12},{20,16},{24,20},{28,24},{1,29},{... | collective-permute-start | bytes 12582920 | tf_op jit(solution)/shard_map/while/body/eval_jaxpr/ppermute | solution.py:9
  351.6 92.3 %copy-start = (f32[2,2,256,2048]{3,2,0,1:T(8,128)S(1)}, f32[2,2,256,2048]{3,2,0,1:T(8,128)}, u32[]{:S(2)}) copy-start(f32[2,2,256,2048]{3,2,0,1:T(8,128)} %get-tuple-element.204) | copy-start | bytes 25165828 | tf_op jit(solution)/shard_map/while
  449.4 3.2 copy-start.1
where the time goes:
time: 491 us; the launch traced here: 490 us
  waiting for transfers between devices  355 us (72%)
  local copies, waits for them, and re-layouts  38.8 us (8%)
  blocking collectives  30.6 us (6%)
  matrix products  28 us (6%)
  starting transfers between devices  21.6 us (4%)
  other arithmetic  15.3 us (3%)
    ppermute x4, waiting for transfers between devices, passed_along(): return lax.ppermute(x, axis, [(i, (i + by) % size) for i in range(size)])  355 us
    while x20, local copies, waits for them, and re-layouts  31.6 us
    dot_general x5, matrix products, block_product(): jnp.einsum('ocfin,cfnx->ofix', weights_block, arriving, preferred_element...  28 us
    psum x1, blocking collectives, body(): raw_kernel = lax.psum(partial_kernel, 'stn')  22.6 us
    ppermute x4, starting transfers between devices, passed_along(): return lax.ppermute(x, axis, [(i, (i + by) % size) for i in range(size)])  21.6 us
  transfers between devices with their start and end apart: 4, of which 4 were waited for; matrix products, arithmetic and copies ran while one was open for 0% of the time, Pallas kernels for 0%

commit v1 on v0

--- a/solution.py
+++ b/solution.py
@@ -1,7 +1,363 @@
+import functools
+
 import jax
 import jax.numpy as jnp
 from jax import lax
+from jax.experimental import pallas as pl
+from jax.experimental.pallas import tpu as pltpu
 from jax.sharding import PartitionSpec as P
+
+MESH = pl.DeviceIdType.MESH
+LANES = 128
+
+
+def remote(src, dst, send_sem, recv_sem, target):
+    return pltpu.make_async_remote_copy(
+        src_ref=src, dst_ref=dst, send_sem=send_sem, recv_sem=recv_sem,
+        device_id=target, device_id_type=MESH,
+    )
+
+
+def ring_kernel(
+    n, n_freq, h, stations, chunk, nq, blocked,
+    greens, weights, out,
+    g_own, g_pair, near, far, w_own, w_pair, acc, red, max_out, max_in,
+    own_sem, w_own_sem, pair_send, pair_recv, wp_send, wp_recv, sib_sem,
+    in_send, in_recv, out_send, far_recv, red_send, red_recv, max_sem,
+):
+    m = n // 2
+    side_len = m // 2
+    sub = chunk // LANES
+    half_rows = h // 2
+    me = lax.axis_index("stn")
+    core = lax.axis_index("pts")
+    fq = lax.axis_index("freq")
+    parity = lax.rem(me, 2)
+    z = me // 2
+    hi = (z >= side_len).astype(jnp.int32)
+    edge = jnp.where(hi == 1, m - 1 - z, z)
+    inward = jnp.where(hi == 1, -2, 2)
+    inner = edge == side_len - 1
+    s_base = hi * nq
+    r_base = (1 - hi) * nq
+    pair_dev = {"stn": me + 1 - 2 * parity}
+    in_dev = {"stn": me + inward}
+    out_dev = {"stn": me - inward}
+    n_far = side_len * 2 * nq
+    n_near = edge * 4 * nq
+    n_near_max = (side_len - 1) * 4 * nq
+    steps = max(n_far, n_near_max, 3 * nq + 1)
+    catch_up = max((steps * 25) // 32, 3 * nq)
+    per_step = -(-steps // (steps - catch_up))
+
+    def columns(q):
+        return pl.ds(pl.multiple_of(q * chunk, LANES), chunk)
+
+    def w_src(freq, j, rows):
+        if blocked:
+            return weights.at[:, freq, j, rows, :]
+        return weights.at[:, freq, rows, pl.ds(pl.multiple_of(j * h, LANES), h)]
+
+    def global_block(e, opposite):
+        low = jnp.where(opposite, 1 - hi, hi) == 0
+        return jnp.where(low, e, m - 1 - e)
+
+    def near_slot(receiver_edge, p, half, b, c):
+        return ((p * 2 + half) * receiver_edge + (receiver_edge - 1 - b)) * nq + c
+
+    def far_slot(p, b, c):
+        return (p * side_len + (side_len - 1 - b)) * nq + c
+
+    def send_inward(src, p, half, b, c):
+        q = jnp.where(half == 0, s_base, r_base) + c
+
+        if side_len > 1:
+            @pl.when(jnp.logical_not(inner))
+            def _():
+                slot = near_slot(edge + 1, p, half, b, c)
+                remote(src, near.at[b, p, q], in_send.at[slot], in_recv.at[slot], in_dev).start()
+
+        @pl.when(jnp.logical_and(inner, half == 0))
+        def _():
+            slot = far_slot(p, b, c)
+            remote(src, far.at[b, p, c], in_send.at[slot], far_recv.at[slot], in_dev).start()
+
+    every_row = pl.ds(0, h)
+    pair_rows = pl.ds(pl.multiple_of(core * half_rows, 8), half_rows)
+
+    def pair_q(i):
+        return jnp.where(i < nq, s_base + i, r_base + i - nq)
+
+    def pair_copy(i):
+        q = pair_q(i)
+        return remote(
+            greens.at[:, 1 - parity, :, columns(q)], g_pair.at[q],
+            pair_send.at[i], pair_recv.at[i], pair_dev,
+        )
+
+    def w_pair_copy(j):
+        return remote(
+            w_src(1 - parity, j, pair_rows), w_pair.at[j, :, pair_rows, :],
+            wp_send.at[j], wp_recv.at[j], pair_dev,
+        )
+
+    def sibling_copy(rows):
+        return remote(
+            w_pair.at[:, :, rows, :], w_pair.at[:, :, rows, :],
+            sib_sem.at[0], sib_sem.at[1], {"pts": 1 - core},
+        )
+
+    def own_copy(q):
+        return pltpu.make_async_copy(
+            greens.at[:, parity, :, columns(q)], g_own.at[q], own_sem.at[q]
+        )
+
+    def w_own_copy(j):
+        return pltpu.make_async_copy(w_src(parity, j, every_row), w_own.at[j], w_own_sem.at[j])
+
+    @pl.loop(0, 2 * nq)
+    def _(i):
+        pair_copy(i).start()
+        half = i // nq
+        c = lax.rem(i, nq)
+        send_inward(greens.at[:, parity, :, columns(pair_q(i))], 0, half, edge, c)
+        own_copy(i).start()
+
+    @pl.loop(0, n)
+    def _(j):
+        w_pair_copy(j).start()
+        w_own_copy(j).start()
+
+    acc[...] = jnp.zeros_like(acc)
+
+    @pl.loop(0, 2 * nq)
+    def _(q):
+        own_copy(q).wait()
+
+    @pl.loop(0, n)
+    def _(j):
+        w_own_copy(j).wait()
+
+    def contribute(w, gi, gj, q, weight):
+        for s in range(sub):
+            part = slice(s * LANES, (s + 1) * LANES)
+            both = jnp.concatenate([gj[0, :, part], gj[1, :, part]], axis=1)
+            a = jnp.dot(w[0], both, preferred_element_type=jnp.float32)
+            b = jnp.dot(w[1], both, preferred_element_type=jnp.float32)
+            t = gi[0, :, part].astype(jnp.float32) * (a[:, :LANES] - b[:, LANES:])
+            t = t + gi[1, :, part].astype(jnp.float32) * (a[:, LANES:] + b[:, :LANES])
+            t = jnp.sum(t.reshape(h // 8, 8, LANES), axis=0)
+            acc[q * sub + s] += t * weight
+
+    def far_at(t):
+        p = t // (side_len * nq)
+        rest = lax.rem(t, side_len * nq)
+        return p, side_len - 1 - rest // nq, lax.rem(rest, nq)
+
+    def near_at(t):
+        width = jnp.maximum(edge, 1) * nq
+        p = t // (2 * width)
+        half = lax.rem(t // width, 2)
+        rest = lax.rem(t, width)
+        return p, half, jnp.maximum(edge, 1) - 1 - rest // nq, lax.rem(rest, nq)
+
+    def part_of(p):
+        return jnp.where(p == 0, parity, 1 - parity)
+
+    def far_work(t, w, g):
+        p, b, c = far_at(t)
+        q = r_base + c
+        j = global_block(b, True) * 2 + part_of(p)
+        contribute(w.at[j], g.at[q], far.at[b, p, c], q, 2.0)
+
+    def near_work(t, w, g):
+        p, half, b, c = near_at(t)
+        q = jnp.where(half == 0, s_base, r_base) + c
+        j = global_block(b, False) * 2 + part_of(p)
+        contribute(w.at[j], g.at[q], near.at[b, p, q], q, 2.0)
+
+    def far_wait(t):
+        p, b, c = far_at(t)
+        ref = far.at[b, p, c]
+        remote(ref, ref, out_send.at[t], far_recv.at[t], in_dev).wait_recv()
+
+        @pl.when(edge > 0)
+        def _():
+            remote(ref, ref, out_send.at[t], far_recv.at[t], out_dev).start()
+
+    def near_wait(t):
+        p, half, b, c = near_at(t)
+        q = jnp.where(half == 0, s_base, r_base) + c
+        ref = near.at[b, p, q]
+        remote(ref, ref, in_send.at[t], in_recv.at[t], out_dev).wait_recv()
+        send_inward(ref, p, half, b, c)
+
+    @pl.loop(0, steps)
+    def _(t):
+        has_pair = jnp.logical_and(t >= nq, t < 3 * nq)
+
+        @pl.when(has_pair)
+        def _():
+            i = t - nq
+            pair_copy(i).wait_recv()
+            send_inward(g_pair.at[pair_q(i)], 1, i // nq, edge, lax.rem(i, nq))
+
+        @pl.when(t < n_far)
+        def _():
+            far_wait(t)
+
+        if side_len > 1:
+            @pl.when(t < n_near)
+            def _():
+                near_wait(t)
+
+        @pl.when(t == catch_up - 1)
+        def _():
+            @pl.loop(0, n)
+            def _(j):
+                w_pair_copy(j).wait_recv()
+
+            sibling_copy(pair_rows).start()
+
+        @pl.when(t < 2 * nq)
+        def _():
+            contribute(w_own.at[2 * z + parity], g_own.at[t], g_own.at[t], t, 1.0)
+
+        @pl.when(has_pair)
+        def _():
+            q = pair_q(t - nq)
+            contribute(w_own.at[2 * z + 1 - parity], g_own.at[q], g_pair.at[q], q, 2.0)
+
+        @pl.when(t < n_far)
+        def _():
+            far_work(t, w_own, g_own)
+
+        if side_len > 1:
+            @pl.when(t < n_near)
+            def _():
+                near_work(t, w_own, g_own)
+
+        @pl.when(t == catch_up)
+        def _():
+            sibling_copy(pl.ds(pl.multiple_of((1 - core) * half_rows, 8), half_rows)).wait_recv()
+
+        @pl.when(t >= catch_up)
+        def _():
+            first = (t - catch_up) * per_step
+
+            @pl.loop(first, jnp.minimum(first + per_step, steps))
+            def _(u):
+                @pl.when(u < 2 * nq)
+                def _():
+                    contribute(w_pair.at[2 * z + 1 - parity], g_pair.at[u], g_pair.at[u], u, 1.0)
+
+                @pl.when(u < n_far)
+                def _():
+                    far_work(u, w_pair, g_pair)
+
+                if side_len > 1:
+                    @pl.when(u < n_near)
+                    def _():
+                        near_work(u, w_pair, g_pair)
+
+    total = n * n_freq
+    rank = me * n_freq + fq
+    red[rank] = jnp.sum(acc[...], axis=1) / stations
+
+    def share_copy(k, source):
+        target = lax.rem(rank + k, total)
+        return remote(
+            red.at[source], red.at[source], red_send.at[k - 1], red_recv.at[k - 1],
+            {"stn": target // n_freq, "freq": lax.rem(target, n_freq)},
+        )
+
+    @pl.loop(1, total)
+    def _(k):
+        share_copy(k, rank).start()
+
+    @pl.loop(1, total)
+    def _(k):
+        share_copy(k, lax.rem(rank - k + total, total)).wait_recv()
+
+    raw = red[0]
+    for d in range(1, total):
+        raw = raw + red[d]
+    max_out[...] = jnp.broadcast_to(jnp.max(jnp.abs(raw)), max_out.shape)
+    max_copy = remote(max_out, max_in, max_sem.at[0], max_sem.at[1], {"pts": 1 - core})
+    max_copy.start()
+
+    @pl.loop(1, total)
+    def _(k):
+        share_copy(k, rank).wait_send()
+
+    @pl.loop(0, 2 * nq)
+    def _(i):
+        pair_copy(i).wait_send()
+
+    @pl.loop(0, n)
+    def _(j):
+        w_pair_copy(j).wait_send()
+
+    sibling_copy(pair_rows).wait_send()
+    ref = far.at[0, 0, 0]
+
+    @pl.loop(0, jnp.where(inner, n_far, (edge + 1) * 4 * nq))
+    def _(t):
+        remote(ref, ref, in_send.at[t], far_recv.at[0], in_dev).wait_send()
+
+    @pl.when(edge > 0)
+    def _():
+        @pl.loop(0, n_far)
+        def _(t):
+            remote(ref, ref, out_send.at[t], far_recv.at[0], out_dev).wait_send()
+
+    max_copy.wait()
+    largest = jnp.maximum(max_out[0:1, 0:1], max_in[0:1, 0:1])
+    out[...] = raw / (largest + 1e-6)
+
+
+def kernel_body(n, n_freq, greens, weights):
+    _, _, h, points = greens.shape
+    stations = weights.shape[3]
+    half = points // 2
+    chunk = LANES
+    while chunk * 2 * h <= 32768 and half % (chunk * 2) == 0:
+        chunk *= 2
+    nq = half // chunk
+    side_len = n // 4
+    n_far = side_len * 2 * nq
+    n_near = max(side_len - 1, 1) * 4 * nq
+    blocked = h % LANES != 0
+    if blocked:
+        weights = weights.reshape(2, weights.shape[1], h, n, h).swapaxes(2, 3)
+    dma = pltpu.SemaphoreType.DMA
+    bf16, f32 = jnp.bfloat16, jnp.float32
+    rows = points // LANES
+    out = pl.pallas_call(
+        functools.partial(ring_kernel, n, n_freq, h, stations, chunk, nq, blocked),
+        out_shape=jax.ShapeDtypeStruct((rows, LANES), f32),
+        in_specs=[pl.BlockSpec(memory_space=pl.ANY)] * 2,
+        out_specs=pl.BlockSpec(memory_space=pltpu.VMEM),
+        scratch_shapes=[
+            pltpu.VMEM((2 * nq, 2, h, chunk), bf16),
+            pltpu.VMEM((2 * nq, 2, h, chunk), bf16),
+            pltpu.VMEM((max(side_len - 1, 1), 2, 2 * nq, 2, h, chunk), bf16),
+            pltpu.VMEM((side_len, 2, nq, 2, h, chunk), bf16),
+            pltpu.VMEM((n, 2, h, h), bf16),
+            pltpu.VMEM((n, 2, h, h), bf16),
+            pltpu.VMEM((rows, 8, LANES), f32),
+            pltpu.VMEM((n * n_freq, rows, LANES), f32),
+            pltpu.VMEM((8, LANES), f32),
+            pltpu.VMEM((8, LANES), f32),
+            dma((2 * nq,)), dma((n,)), dma((2 * nq,)), dma((2 * nq,)), dma((n,)), dma((n,)), dma((2,)),
+            dma((max(n_near, n_far),)), dma((n_near,)), dma((n_far,)), dma((n_far,)),
+            dma((n * n_freq - 1,)), dma((n * n_freq - 1,)), dma((2,)),
+        ],
+        compiler_params=pltpu.CompilerParams(
+            has_side_effects=True, vmem_limit_bytes=60 * 1024 * 1024
+        ),
+    )(greens, weights)
+    return out.reshape(points)
 
 
 def passed_along(x, axis, by):
@@ -52,6 +408,14 @@
 
 
 def solution(mesh):
+    n, cores, n_freq = mesh.shape["stn"], mesh.shape["pts"], mesh.shape["freq"]
+
+    def either(greens, noise_weights):
+        _, freqs, rows, points = greens.shape
+        fits = n % 4 == 0 and cores == 2 and freqs == 2 and rows % 32 == 0 and points % (2 * LANES) == 0
+        if fits:
+            return kernel_body(n, n_freq, greens, noise_weights)
+        return body(greens, noise_weights)
+
     in_specs = (P(None, "freq", "stn", "pts"), P(None, "freq", "stn", None))
-    out_specs = P("pts")
-    return jax.shard_map(body, mesh=mesh, in_specs=in_specs, out_specs=out_specs, check_vma=False)
+    return jax.shard_map(either, mesh=mesh, in_specs=in_specs, out_specs=P("pts"), check_vma=False)

time: 491 us -> 124 us (0.25)
  waiting for transfers between devices: 355 us -> 0 us
  Pallas kernels: 0 us -> 122 us
  local copies, waits for them, and re-layouts: 38.8 us -> 1.3 us
  blocking collectives: 30.6 us -> 0 us
  matrix products: 28 us -> 0 us
  starting transfers between devices: 21.6 us -> 0 us
  other arithmetic: 15.3 us -> 0 us
    ppermute x4 -> x0, waiting for transfers between devices: 355 us -> none  [passed_along(): return lax.ppermute(x, axis, [(i, (i + by) % size) for i in range(size)])]
    pallas_call x0 -> x1, Pallas kernels: none -> 122 us  [kernel_body(): pl.pallas_call(functools.partial(ring_kernel, n, n_freq, h, stations, chu...]
    while x20 -> x0, local copies, waits for them, and re-layouts: 31.6 us -> none
    dot_general x5 -> x0, matrix products: 28 us -> none  [block_product(): jnp.einsum('ocfin,cfnx->ofix', weights_block, arriving, preferred_element...]
    psum x2 -> x0, blocking collectives: 27.6 us -> none  [the longest x1 22.6 us: body(): raw_kernel = lax.psum(partial_kernel, 'stn')]
    ppermute x4 -> x0, starting transfers between devices: 21.6 us -> none  [passed_along(): return lax.ppermute(x, axis, [(i, (i + by) % size) for i in range(size)])]
    another operation x2 -> x0, other arithmetic: 6.94 us -> none  [mixing_of(): jnp.stack([jnp.stack([weights[0], negated]), jnp.stack([weights[1], weigh...]
    unnamed x8 -> x1, local copies, waits for them, and re-layouts: 7.14 us -> 1.3 us
  transfers between devices with their start and end apart: 4 -> 0, of which waited for: 4 -> 0; matrix products, arithmetic and copies ran while one was open for 0% -> 0% of each run, Pallas kernels for 0% -> 0%
where the time goes in v1:
time: 124 us; the launch traced here: 123 us
  Pallas kernels  122 us (98%)
  local copies, waits for them, and re-layouts  1.3 us (1%)
    pallas_call x1, Pallas kernels, kernel_body(): pl.pallas_call(functools.partial(ring_kernel, n, n_freq, h, stations, chu...  122 us

profile of v1, /device:TPU:0, one launch (start us, length us, event | category | flops | bytes accessed | tf_op | source)
XLA Modules:
  0.0 123.3 jit_solution(9071484582064811759)
XLA Ops:
  0.0 122.0 %shard_map.28 = f32[16,128]{1,0:T(8,128)} custom-call(bf16[2,2,256,2048]{3,2,1,0:T(8,128)(2,1)} %greens.1, bf16[2,2,256,2048]{3,2,1,0:T(8,128)(2,1)} %weights.1), custom_call_target="tpu_custom_call" | custom-call | tf_op jit(solution)/shard_map/pallas_call | solution.py:336
  122.0 1.3 %copy.4 = f32[2048]{0:T(1024)} copy(f32[2048]{0:T(1024)} %bitcast.1) | data formatting | bytes 16384

commit v2 on v1

--- a/solution.py
+++ b/solution.py
@@ -23,7 +23,7 @@
     greens, weights, out,
     g_own, g_pair, near, far, w_own, w_pair, acc, red, max_out, max_in,
     own_sem, w_own_sem, pair_send, pair_recv, wp_send, wp_recv, sib_sem,
-    in_send, in_recv, out_send, far_recv, red_send, red_recv, max_sem,
+    in_send, in_recv, out_send, far_recv, red_send, red_recv, max_sem, hello_sem, pair_hello,
 ):
     m = n // 2
     side_len = m // 2
@@ -46,8 +46,10 @@
     n_far = side_len * 2 * nq
     n_near = edge * 4 * nq
     n_near_max = (side_len - 1) * 4 * nq
-    steps = max(n_far, n_near_max, 3 * nq + 1)
-    catch_up = max((steps * 25) // 32, 3 * nq)
+    steps = max(n_far, n_near_max, 3 * nq + 2)
+    spread = side_len == 2
+    catch_up = 2 * nq + 1 if spread else max((steps * 25) // 32, 3 * nq + 1)
+    left = steps - catch_up
     per_step = -(-steps // (steps - catch_up))
 
     def columns(q):
@@ -82,6 +84,45 @@
             slot = far_slot(p, b, c)
             remote(src, far.at[b, p, c], in_send.at[slot], far_recv.at[slot], in_dev).start()
 
+    freq_dev = {"freq": n_freq - 1 - fq}
+    barrier = pltpu.get_barrier_semaphore()
+    up, down = z < m - 1, z > 0
+    greeted = [pair_dev, {"pts": 1 - core}, freq_dev]
+
+    def greet(sem, device):
+        pl.semaphore_signal(sem, inc=1, device_id=device, device_id_type=MESH)
+
+    def along_z(sem_down, sem_up):
+        @pl.when(up)
+        def _():
+            greet(sem_up, {"stn": me + 2})
+
+        @pl.when(down)
+        def _():
+            greet(sem_down, {"stn": me - 2})
+
+    for device in greeted:
+        greet(barrier, device)
+    along_z(barrier, barrier)
+    pl.semaphore_wait(barrier, len(greeted) + up.astype(jnp.int32) + down.astype(jnp.int32))
+
+    def hello():
+        @pl.loop(0, m - 1)
+        def _(r):
+            along_z(hello_sem.at[0, r], hello_sem.at[1, r])
+
+            @pl.when(up)
+            def _():
+                pl.semaphore_wait(hello_sem.at[0, r], 1)
+
+            @pl.when(down)
+            def _():
+                pl.semaphore_wait(hello_sem.at[1, r], 1)
+
+        for i, device in enumerate((pair_dev, freq_dev)):
+            greet(pair_hello.at[i], device)
+            pl.semaphore_wait(pair_hello.at[i], 1)
+
     every_row = pl.ds(0, h)
     pair_rows = pl.ds(pl.multiple_of(core * half_rows, 8), half_rows)
 
@@ -117,7 +158,10 @@
 
     @pl.loop(0, 2 * nq)
     def _(i):
-        pair_copy(i).start()
+        @pl.when(i < nq)
+        def _():
+            pair_copy(i).start()
+
         half = i // nq
         c = lax.rem(i, nq)
         send_inward(greens.at[:, parity, :, columns(pair_q(i))], 0, half, edge, c)
@@ -128,6 +172,12 @@
         w_pair_copy(j).start()
         w_own_copy(j).start()
 
+    @pl.loop(nq, 2 * nq)
+    def _(i):
+        pair_copy(i).start()
+
+    hello()
+
     acc[...] = jnp.zeros_like(acc)
 
     @pl.loop(0, 2 * nq)
@@ -142,8 +192,8 @@
         for s in range(sub):
             part = slice(s * LANES, (s + 1) * LANES)
             both = jnp.concatenate([gj[0, :, part], gj[1, :, part]], axis=1)
-            a = jnp.dot(w[0], both, preferred_element_type=jnp.float32)
-            b = jnp.dot(w[1], both, preferred_element_type=jnp.float32)
+            ab = jnp.dot(w[...].reshape(2 * h, h), both, preferred_element_type=jnp.float32)
+            a, b = ab[:h], ab[h:]
             t = gi[0, :, part].astype(jnp.float32) * (a[:, :LANES] - b[:, LANES:])
             t = t + gi[1, :, part].astype(jnp.float32) * (a[:, LANES:] + b[:, :LANES])
             t = jnp.sum(t.reshape(h // 8, 8, LANES), axis=0)
@@ -192,13 +242,21 @@
         remote(ref, ref, in_send.at[t], in_recv.at[t], out_dev).wait_recv()
         send_inward(ref, p, half, b, c)
 
+    def newest(u):
+        far_work(u, w_pair, g_pair)
+
+        @pl.when(u < n_near)
+        def _():
+            near_work(u, w_pair, g_pair)
+
     @pl.loop(0, steps)
     def _(t):
-        has_pair = jnp.logical_and(t >= nq, t < 3 * nq)
+        has_pair = jnp.logical_and(jnp.logical_and(t >= nq, t <= 3 * nq), t != 2 * nq)
+        turn = t - nq - (t > 2 * nq).astype(jnp.int32)
 
         @pl.when(has_pair)
         def _():
-            i = t - nq
+            i = turn
             pair_copy(i).wait_recv()
             send_inward(g_pair.at[pair_q(i)], 1, i // nq, edge, lax.rem(i, nq))
 
@@ -225,7 +283,7 @@
 
         @pl.when(has_pair)
         def _():
-            q = pair_q(t - nq)
+            q = pair_q(turn)
             contribute(w_own.at[2 * z + 1 - parity], g_own.at[q], g_pair.at[q], q, 2.0)
 
         @pl.when(t < n_far)
@@ -244,21 +302,35 @@
         @pl.when(t >= catch_up)
         def _():
             first = (t - catch_up) * per_step
-
-            @pl.loop(first, jnp.minimum(first + per_step, steps))
+            last = jnp.minimum(first + per_step, steps)
+            if spread:
+                first = ((t - catch_up) * 2 * nq) // left
+                last = ((t - catch_up + 1) * 2 * nq) // left
+
+            @pl.loop(first, last)
             def _(u):
                 @pl.when(u < 2 * nq)
                 def _():
-                    contribute(w_pair.at[2 * z + 1 - parity], g_pair.at[u], g_pair.at[u], u, 1.0)
-
-                @pl.when(u < n_far)
-                def _():
-                    far_work(u, w_pair, g_pair)
+                    q = pair_q(u)
+                    contribute(w_pair.at[2 * z + 1 - parity], g_pair.at[q], g_pair.at[q], q, 1.0)
+
+                if spread:
+                    far_work(lax.rem(u, side_len) * nq + u // side_len, w_pair, g_pair)
+                else:
+                    @pl.when(u < n_far)
+                    def _():
+                        far_work(u, w_pair, g_pair)
 
                 if side_len > 1:
                     @pl.when(u < n_near)
                     def _():
                         near_work(u, w_pair, g_pair)
+
+            if spread:
+                newest(t - 1)
+
+    if spread:
+        newest(steps - 1)
 
     total = n * n_freq
     rank = me * n_freq + fq
@@ -352,9 +424,10 @@
             dma((2 * nq,)), dma((n,)), dma((2 * nq,)), dma((2 * nq,)), dma((n,)), dma((n,)), dma((2,)),
             dma((max(n_near, n_far),)), dma((n_near,)), dma((n_far,)), dma((n_far,)),
             dma((n * n_freq - 1,)), dma((n * n_freq - 1,)), dma((2,)),
+            pltpu.SemaphoreType.REGULAR((2, n // 2 - 1)), pltpu.SemaphoreType.REGULAR((2,)),
         ],
         compiler_params=pltpu.CompilerParams(
-            has_side_effects=True, vmem_limit_bytes=60 * 1024 * 1024
+            collective_id=0, has_side_effects=True, vmem_limit_bytes=60 * 1024 * 1024
         ),
     )(greens, weights)
     return out.reshape(points)
@@ -412,7 +485,7 @@
 
     def either(greens, noise_weights):
         _, freqs, rows, points = greens.shape
-        fits = n % 4 == 0 and cores == 2 and freqs == 2 and rows % 32 == 0 and points % (2 * LANES) == 0
+        fits = n % 4 == 0 and cores == 2 and freqs == 2 and n_freq == 2 and rows % 32 == 0 and points % (2 * LANES) == 0
         if fits:
             return kernel_body(n, n_freq, greens, noise_weights)
         return body(greens, noise_weights)

time: 124 us -> 113 us (0.911)
  Pallas kernels: 122 us -> 112 us
    pallas_call x1, Pallas kernels: 122 us -> 112 us  [kernel_body(): pl.pallas_call(functools.partial(ring_kernel, n, n_freq, h, stations, chu...]
where the time goes in v2:
time: 113 us
  Pallas kernels  112 us (99%)
  local copies, waits for them, and re-layouts  1.3 us (1%)
    pallas_call x1, Pallas kernels, kernel_body(): pl.pallas_call(functools.partial(ring_kernel, n, n_freq, h, stations, chu...  112 us

profile of v2, /device:TPU:0, one launch (start us, length us, event | category | flops | bytes accessed | tf_op | source)
XLA Modules:
  0.0 113.2 jit_solution(8051481320211434854)
XLA Ops:
  0.0 111.9 %shard_map.28 = f32[16,128]{1,0:T(8,128)} custom-call(bf16[2,2,256,2048]{3,2,1,0:T(8,128)(2,1)} %greens.1, bf16[2,2,256,2048]{3,2,1,0:T(8,128)(2,1)} %weights.1), custom_call_target="tpu_custom_call" | custom-call | tf_op jit(solution)/shard_map/pallas_call | solution.py:408
  111.9 1.3 %copy.4 = f32[2048]{0:T(1024)} copy(f32[2048]{0:T(1024)} %bitcast.1) | data formatting | bytes 16384

commit v3 on v2

--- a/solution.py
+++ b/solution.py
@@ -70,6 +70,9 @@
     def far_slot(p, b, c):
         return (p * side_len + (side_len - 1 - b)) * nq + c
 
+    def piece(k):
+        return pl.ds(k * half_rows, half_rows)
+
     def send_inward(src, p, half, b, c):
         q = jnp.where(half == 0, s_base, r_base) + c
 
@@ -77,12 +80,16 @@
             @pl.when(jnp.logical_not(inner))
             def _():
                 slot = near_slot(edge + 1, p, half, b, c)
-                remote(src, near.at[b, p, q], in_send.at[slot], in_recv.at[slot], in_dev).start()
+                remote(src, near.at[b, p, q], in_send.at[slot, 0], in_recv.at[slot], in_dev).start()
 
         @pl.when(jnp.logical_and(inner, half == 0))
         def _():
             slot = far_slot(p, b, c)
-            remote(src, far.at[b, p, c], in_send.at[slot], far_recv.at[slot], in_dev).start()
+            for k in range(2):
+                remote(
+                    src.at[:, piece(k), :], far.at[b, p, c, :, piece(k), :],
+                    in_send.at[slot, k], far_recv.at[slot, k], in_dev,
+                ).start()
 
     freq_dev = {"freq": n_freq - 1 - fq}
     barrier = pltpu.get_barrier_semaphore()
@@ -228,18 +235,19 @@
 
     def far_wait(t):
         p, b, c = far_at(t)
-        ref = far.at[b, p, c]
-        remote(ref, ref, out_send.at[t], far_recv.at[t], in_dev).wait_recv()
-
-        @pl.when(edge > 0)
-        def _():
-            remote(ref, ref, out_send.at[t], far_recv.at[t], out_dev).start()
+        for k in range(2):
+            ref = far.at[b, p, c, :, piece(k), :]
+            remote(ref, ref, out_send.at[t, k], far_recv.at[t, k], in_dev).wait_recv()
+
+            @pl.when(edge > 0)
+            def _():
+                remote(ref, ref, out_send.at[t, k], far_recv.at[t, k], out_dev).start()
 
     def near_wait(t):
         p, half, b, c = near_at(t)
         q = jnp.where(half == 0, s_base, r_base) + c
         ref = near.at[b, p, q]
-        remote(ref, ref, in_send.at[t], in_recv.at[t], out_dev).wait_recv()
+        remote(ref, ref, in_send.at[t, 0], in_recv.at[t], out_dev).wait_recv()
         send_inward(ref, p, half, b, c)
 
     def newest(u):
@@ -371,17 +379,29 @@
         w_pair_copy(j).wait_send()
 
     sibling_copy(pair_rows).wait_send()
-    ref = far.at[0, 0, 0]
-
-    @pl.loop(0, jnp.where(inner, n_far, (edge + 1) * 4 * nq))
-    def _(t):
-        remote(ref, ref, in_send.at[t], far_recv.at[0], in_dev).wait_send()
+    whole = far.at[0, 0, 0]
+    parts = [far.at[0, 0, 0, :, piece(k), :] for k in range(2)]
+
+    @pl.when(inner)
+    def _():
+        @pl.loop(0, n_far)
+        def _(t):
+            for k in range(2):
+                remote(parts[k], parts[k], in_send.at[t, k], far_recv.at[0, k], in_dev).wait_send()
+
+    if side_len > 1:
+        @pl.when(jnp.logical_not(inner))
+        def _():
+            @pl.loop(0, (edge + 1) * 4 * nq)
+            def _(t):
+                remote(whole, whole, in_send.at[t, 0], far_recv.at[0, 0], in_dev).wait_send()
 
     @pl.when(edge > 0)
     def _():
         @pl.loop(0, n_far)
         def _(t):
-            remote(ref, ref, out_send.at[t], far_recv.at[0], out_dev).wait_send()
+            for k in range(2):
+                remote(parts[k], parts[k], out_send.at[t, k], far_recv.at[0, k], out_dev).wait_send()
 
     max_copy.wait()
     largest = jnp.maximum(max_out[0:1, 0:1], max_in[0:1, 0:1])
@@ -422,7 +442,7 @@
             pltpu.VMEM((8, LANES), f32),
             pltpu.VMEM((8, LANES), f32),
             dma((2 * nq,)), dma((n,)), dma((2 * nq,)), dma((2 * nq,)), dma((n,)), dma((n,)), dma((2,)),
-            dma((max(n_near, n_far),)), dma((n_near,)), dma((n_far,)), dma((n_far,)),
+            dma((max(n_near, n_far), 2)), dma((n_near,)), dma((n_far, 2)), dma((n_far, 2)),
             dma((n * n_freq - 1,)), dma((n * n_freq - 1,)), dma((2,)),
             pltpu.SemaphoreType.REGULAR((2, n // 2 - 1)), pltpu.SemaphoreType.REGULAR((2,)),
         ],

time: 113 us -> 114 us (level)
  no operation moved by 1% of the time
where the time goes in v3:
time: 114 us
  Pallas kernels  112 us (98%)
  local copies, waits for them, and re-layouts  1.3 us (1%)
    pallas_call x1, Pallas kernels, kernel_body(): pl.pallas_call(functools.partial(ring_kernel, n, n_freq, h, stations, chu...  112 us

profile of v3, /device:TPU:0, one launch (start us, length us, event | category | flops | bytes accessed | tf_op | source)
XLA Modules:
  0.0 113.7 jit_solution(11550658135050475444)
XLA Ops:
  0.0 112.4 %shard_map.28 = f32[16,128]{1,0:T(8,128)} custom-call(bf16[2,2,256,2048]{3,2,1,0:T(8,128)(2,1)} %greens.1, bf16[2,2,256,2048]{3,2,1,0:T(8,128)(2,1)} %weights.1), custom_call_target="tpu_custom_call" | custom-call | tf_op jit(solution)/shard_map/pallas_call | solution.py:428
  112.4 1.3 %copy.4 = f32[2048]{0:T(1024)} copy(f32[2048]{0:T(1024)} %bitcast.1) | data formatting | bytes 16384
